TPU v7x, 256 devices: a whole 4x4x8 slice. The times are simulated.
256 devices in a mesh: tx: 8 (over x_lo, y), ty: 8 (over z), lev: 4 (over x_hi, core).
Axes of the slice: x: 4 (x_hi: 2, x_lo: 2; x = x_hi * 2 + x_lo), y: 4, z: 8, core: 2. Of those that a mesh axis runs over, the one named last changes fastest.
Arguments:
- members: bfloat16 [8, 512, 128, 128], P('lev', 'tx', 'ty'), may hold values from -6 to 6
- obs_pert: bfloat16 [65536, 128], P(('tx', 'ty', 'lev')), may hold values from -6 to 6
- innovation: bfloat16 [65536], P(('tx', 'ty', 'lev')), may hold values from -6 to 6
- obs_precision: bfloat16 [65536], P(('tx', 'ty', 'lev')), may hold values from 0.25 to 4
- obs_owner: int32 [32, 8, 256], P('tx', 'ty'), may hold values from 0 to 63, as said below
- obs_slot: int32 [32, 8, 256], P('tx', 'ty'), may hold values from 0 to 1023
- obs_count: int32 [32, 8], P('tx', 'ty'), may hold values from 64 to 256
- local_weight: float32 [32, 8, 256], P('tx', 'ty'), may hold values from 0.05 to 1
Outputs:
- analysis: bfloat16 [8, 512, 128, 128], P('lev', 'tx', 'ty')
Inputs may be any that keep to these rules, and one draw needn't show every extreme that they name: `obs_owner`: the tile numbered tx index times the number of ty tiles plus ty index; it is the coarse column's own tile or one of the tiles beside it, diagonals included. `obs_count`: slots at and beyond a coarse column's count are padding.
All inputs are finite; a program needn't handle non-finite values.
Results may differ from a plain program's by a relative error of at most 0.0054.
Values may be sent and summed in bfloat16 or wider, within the bound.
A program may use at most 64 MiB of HBM per device.

v0:
```python
import jax
import jax.numpy as jnp
from jax import lax
from jax.sharding import PartitionSpec as P

SPACING = 16
NS_STEPS = 4


def rows_first(arrays, axis, dims):
    turned = [jnp.moveaxis(a, dim, 0) for a, dim in zip(arrays, dims)]
    widths = [t[0].size for t in turned]
    both = jnp.concatenate([t.reshape(-1, w) for t, w in zip(turned, widths)], axis=1)
    out = lax.all_gather(both, axis, axis=0, tiled=True)
    parts = jnp.split(out, [sum(widths[:k]) for k in range(1, len(widths))], axis=1)
    return tuple(
        (
            jnp.moveaxis(b.reshape(-1, *t.shape[1:]), 0, dim)
            for b, t, dim in zip(parts, turned, dims)
        )
    )


def padded(array, sides, width):
    for axis, dim in sides:
        size, length = (lax.axis_size(axis), array.shape[dim])
        up = [(i, (i + 1) % size) for i in range(size - 1)]
        down = [(j, i) for i, j in up]
        last = lax.slice_in_dim(array, length - width, length, axis=dim)
        initial = lax.slice_in_dim(array, 0, width, axis=dim)
        before = lax.ppermute(last, axis, up)
        after = lax.ppermute(initial, axis, down)
        array = jnp.concatenate([before, array, after], axis=dim)
    return array


def finish_solve(gram_matrix, projected):
    member_count = gram_matrix.shape[1]
    spread = float(member_count - 1)
    identity = jnp.eye(member_count, dtype=jnp.float32)
    scale_norm = spread + jnp.sqrt(jnp.sum(gram_matrix * gram_matrix, axis=(1, 2)))
    sqrt_iter = (spread * identity + gram_matrix) / scale_norm[:, None, None]
    inv_iter = jnp.broadcast_to(identity, sqrt_iter.shape)
    for iteration in range(NS_STEPS):
        middle = 1.5 * identity - 0.5 * jnp.einsum(
            "bij,bjk->bik", inv_iter, sqrt_iter, precision=lax.Precision.HIGHEST
        )
        sqrt_iter = jnp.einsum("bij,bjk->bik", sqrt_iter, middle, precision=lax.Precision.HIGHEST)
        inv_iter = jnp.einsum("bij,bjk->bik", middle, inv_iter, precision=lax.Precision.HIGHEST)
    inner = jnp.einsum("bij,bj->bi", inv_iter, projected, precision=lax.Precision.HIGHEST)
    mean_weights = (
        jnp.einsum("bij,bj->bi", inv_iter, inner, precision=lax.Precision.HIGHEST)
        / scale_norm[:, None]
    )
    transform = (jnp.sqrt(spread) / jnp.sqrt(scale_norm))[:, None, None] * inv_iter + mean_weights[
        :, :, None
    ]
    return transform.astype(jnp.bfloat16)


def fractions(count, half_span):
    place = jnp.arange(count)[:, None]
    within = jnp.arange(half_span)[None, :].astype(jnp.float32)
    return jnp.where(
        place % 2 == 0,
        (within + half_span + 0.5) / (2 * half_span),
        (within + 0.5) / (2 * half_span),
    )


def solve_columns(lookup, counts, local_part, flat_pert, flat_values):
    column_count, slots = lookup.shape
    member_count = flat_pert.shape[1]
    block_len = min(slots, 128)
    live_blocks = (jnp.max(counts) + block_len - 1) // block_len

    def add_block(block_index, carry):
        gram_matrix, projected = carry
        offset = block_index * block_len
        slot_rows = lax.dynamic_slice_in_dim(lookup, offset, block_len, 1)
        slot_local = lax.dynamic_slice_in_dim(local_part, offset, block_len, 1)
        position = offset + jnp.arange(block_len)
        active = position[None, :] < counts[:, None]
        pert_rows = flat_pert[slot_rows].astype(jnp.float32)
        picked = flat_values[:, slot_rows]
        precision_w = jnp.where(active, picked[1].astype(jnp.float32) * slot_local, 0.0)
        departure = picked[0].astype(jnp.float32)
        gram_matrix = gram_matrix + jnp.einsum(
            "bsk,bsm->bkm",
            pert_rows * precision_w[:, :, None],
            pert_rows,
            precision=lax.Precision.HIGHEST,
        )
        projected = projected + jnp.einsum(
            "bsk,bs->bk", pert_rows, precision_w * departure, precision=lax.Precision.HIGHEST
        )
        return (gram_matrix, projected)

    start_gram = jnp.zeros((column_count, member_count, member_count), jnp.float32)
    start_proj = jnp.zeros((column_count, member_count), jnp.float32)
    gram_matrix, projected = lax.fori_loop(0, live_blocks, add_block, (start_gram, start_proj))
    return finish_solve(gram_matrix, projected)


def clamp_edges(rimmed, axis_index, axis_count, dim):
    lower = jnp.where(
        axis_index == 0,
        lax.slice_in_dim(rimmed, 1, 2, axis=dim),
        lax.slice_in_dim(rimmed, 0, 1, axis=dim),
    )
    last = rimmed.shape[dim]
    upper = jnp.where(
        axis_index == axis_count - 1,
        lax.slice_in_dim(rimmed, last - 2, last - 1, axis=dim),
        lax.slice_in_dim(rimmed, last - 1, last, axis=dim),
    )
    return jnp.concatenate(
        [lower, lax.slice_in_dim(rimmed, 1, last - 1, axis=dim), upper], axis=dim
    )


def per_device(
    members, obs_pert, innovation, obs_precision, obs_owner, obs_slot, obs_count, local_weight
):
    scalars = jnp.stack([innovation, obs_precision])
    tile_pert, tile_values = rows_first((obs_pert, scalars), "lev", (0, 1))
    near_pert, near_values = (
        padded(tile_pert[None, None], (("tx", 0), ("ty", 1)), 1),
        padded(tile_values[None, None], (("tx", 0), ("ty", 1)), 1),
    )
    tile_len = near_pert.shape[2]
    member_count = near_pert.shape[3]
    flat_pert = near_pert.reshape(9 * tile_len, member_count)
    flat_values = jnp.transpose(near_values, (2, 0, 1, 3)).reshape(2, 9 * tile_len)
    column_x = lax.axis_index("tx")
    column_y = lax.axis_index("ty")
    tiles_x = lax.axis_size("tx")
    tiles_y = lax.axis_size("ty")
    near_x = obs_owner // tiles_y - column_x + 1
    near_y = obs_owner % tiles_y - column_y + 1
    lookup = (near_x * 3 + near_y) * tile_len + obs_slot
    coarse_x, coarse_y, slots = lookup.shape
    lookup = lookup.reshape(coarse_x * coarse_y, slots)
    counts = obs_count.reshape(coarse_x * coarse_y)
    local_part = local_weight.reshape(coarse_x * coarse_y, slots)
    weights = solve_columns(lookup, counts, local_part, flat_pert, flat_values)
    weights = weights.reshape(coarse_x, coarse_y, member_count, member_count)
    rimmed = padded(weights, (("tx", 0), ("ty", 1)), 1)
    rimmed = clamp_edges(rimmed, column_x, tiles_x, 0)
    rimmed = clamp_edges(rimmed, column_y, tiles_y, 1)
    doubled = jnp.repeat(jnp.repeat(rimmed, 2, axis=0), 2, axis=1)
    level_count, width_x, width_y, _ = members.shape
    half_span = SPACING // 2
    patch_x = width_x // half_span
    patch_y = width_y // half_span
    frac_x = fractions(patch_x, half_span)
    frac_y = fractions(patch_y, half_span)
    ens_mean = jnp.mean(members, axis=3, keepdims=True, dtype=jnp.float32)
    pert = (members.astype(jnp.float32) - ens_mean).astype(jnp.bfloat16)
    patched = pert.reshape(level_count, patch_x, half_span, patch_y, half_span, member_count)
    summed = jnp.zeros(patched.shape, jnp.float32)
    for upper_x in range(2):
        for upper_y in range(2):
            corner = doubled[
                1 + 2 * upper_x : 1 + 2 * upper_x + patch_x,
                1 + 2 * upper_y : 1 + 2 * upper_y + patch_y,
            ]
            product = jnp.einsum(
                "lxaybi,xyij->lxaybj", patched, corner, preferred_element_type=jnp.float32
            )
            factor_x = frac_x if upper_x == 1 else 1.0 - frac_x
            factor_y = frac_y if upper_y == 1 else 1.0 - frac_y
            summed = (
                summed
                + product
                * factor_x[None, :, :, None, None, None]
                * factor_y[None, None, None, :, :, None]
            )
    return (ens_mean + summed.reshape(members.shape)).astype(jnp.bfloat16)


def solution(mesh):
    placed = (
        P("lev", "tx", "ty", None),
        P(("tx", "ty", "lev"), None),
        P(("tx", "ty", "lev")),
        P(("tx", "ty", "lev")),
        P("tx", "ty", None),
        P("tx", "ty", None),
        P("tx", "ty"),
        P("tx", "ty", None),
    )
    return jax.shard_map(
        per_device,
        mesh=mesh,
        in_specs=placed,
        out_specs=P("lev", "tx", "ty", None),
        check_vma=False,
    )
```

profile of v0, /device:TPU:34, one launch (start us, length us, event | category | flops | bytes accessed | tf_op | source)
XLA Modules:
  0.0 102.1 jit_solution(17852004489440883097)
XLA Ops:
  2.4 8.3 %all_gather.3 = bf16[1024,130]{1,0:T(8,128)(2,1)S(1)} all-gather(bf16[256,130]{1,0:T(8,128)(2,1)S(1)} %pad_maximum_fusion.6), channel_id=1, replica_groups=mesh['tx'=8,'ty'=8,'lev'=4] {'lev'}, dimensions={0}, use_global_device_ids=true | all-gather | bytes 332800 | tf_op jit(solution)/shard_map/all_gather | solution.py:14
  10.7 3.5 %collective-permute-start = (bf16[1,1,1024,128]{3,2,1,0:T(8,128)(2,1)S(1)}, bf16[1,1,1024,128]{3,2,1,0:T(8,128)(2,1)S(1)}, u32[]{:S(2)}, u32[]{:S(2)}) collective-permute-start(bf16[1,1,1024,128]{3,2,1,0:T(8,128)(2,1)S(1)} %slice_bitcast_fusion.11), channel_id=1, source_target_pairs={{0,32},{32,64},{64,96},{96,128},{128,160},{160,192},{192,224},{1,3... | collective-permute-start | bytes 786440 | tf_op jit(solution)/shard_map/ppermute | solution.py:31
  14.2 4.5 %collective-permute-start.1 = (bf16[1,1,1024,128]{3,2,1,0:T(8,128)(2,1)S(1)}, bf16[1,1,1024,128]{3,2,1,0:T(8,128)(2,1)S(1)}, u32[]{:S(2)}, u32[]{:S(2)}) collective-permute-start(bf16[1,1,1024,128]{3,2,1,0:T(8,128)(2,1)S(1)} %slice_bitcast_fusion.11), channel_id=1, source_target_pairs={{32,0},{64,32},{96,64},{128,96},{160,128},{192,160},{224,192},{33,... | collective-permute-start | bytes 786440 | tf_op jit(solution)/shard_map/ppermute | solution.py:32
  18.7 1.9 %collective-permute-start.4 = (bf16[1,1,2,1024]{2,3,1,0:T(8,128)(2,1)S(1)}, bf16[1,1,2,1024]{2,3,1,0:T(8,128)(2,1)}, u32[]{:S(2)}, u32[]{:S(2)}) collective-permute-start(bf16[1,1,2,1024]{2,3,1,0:T(8,128)(2,1)S(1)} %slice_bitcast_fusion.10), channel_id=1, source_target_pairs={{0,32},{32,64},{64,96},{96,128},{128,160},{160,192},{192,224},{1,3... | collective-permute-start | bytes 12296 | tf_op jit(solution)/shard_map/ppermute | solution.py:31
  20.6 6.0 %collective-permute-start.5 = (bf16[1,1,2,1024]{2,3,1,0:T(8,128)(2,1)S(1)}, bf16[1,1,2,1024]{2,3,1,0:T(8,128)(2,1)}, u32[]{:S(2)}, u32[]{:S(2)}) collective-permute-start(bf16[1,1,2,1024]{2,3,1,0:T(8,128)(2,1)S(1)} %slice_bitcast_fusion.10), channel_id=1, source_target_pairs={{32,0},{64,32},{96,64},{128,96},{160,128},{192,160},{224,192},{33,... | collective-permute-start | bytes 12296 | tf_op jit(solution)/shard_map/ppermute | solution.py:32
  28.0 3.8 %collective-permute-start.2 = (bf16[3,1,1024,128]{3,2,1,0:T(8,128)(2,1)S(1)}, bf16[3,1,1024,128]{3,2,1,0:T(8,128)(2,1)S(1)}, u32[]{:S(2)}, u32[]{:S(2)}) collective-permute-start(bf16[3,1,1024,128]{3,2,1,0:T(8,128)(2,1)S(1)} %pad_maximum_fusion.1), channel_id=1, source_target_pairs={{0,4},{4,8},{8,12},{12,16},{16,20},{20,24},{24,28},{1,5},{5,9},{9,... | collective-permute-start | bytes 2359304 | tf_op jit(solution)/shard_map/ppermute | solution.py:31
  31.8 2.1 %collective-permute-start.3 = (bf16[3,1,1024,128]{3,2,1,0:T(8,128)(2,1)S(1)}, bf16[3,1,1024,128]{3,2,1,0:T(8,128)(2,1)}, u32[]{:S(2)}, u32[]{:S(2)}) collective-permute-start(bf16[3,1,1024,128]{3,2,1,0:T(8,128)(2,1)S(1)} %pad_maximum_fusion.1), channel_id=1, source_target_pairs={{4,0},{8,4},{12,8},{16,12},{20,16},{24,20},{28,24},{5,1},{9,5},{13... | collective-permute-start | bytes 2359304 | tf_op jit(solution)/shard_map/ppermute | solution.py:32
  37.4 3.8 %collective-permute-start.6 = (bf16[3,1,2,1024]{3,2,1,0:T(2,128)(2,1)S(1)}, bf16[3,1,2,1024]{3,2,1,0:T(2,128)(2,1)S(1)}, u32[]{:S(2)}, u32[]{:S(2)}) collective-permute-start(bf16[3,1,2,1024]{3,2,1,0:T(2,128)(2,1)S(1)} %pad_maximum_fusion.8), channel_id=1, source_target_pairs={{0,4},{4,8},{8,12},{12,16},{16,20},{20,24},{24,28},{1,5},{5,9},{9,... | collective-permute-start | bytes 36872 | tf_op jit(solution)/shard_map/ppermute | solution.py:31
  41.2 2.1 %collective-permute-start.7 = (bf16[3,1,2,1024]{3,2,1,0:T(2,128)(2,1)S(1)}, bf16[3,1,2,1024]{3,2,1,0:T(2,128)(2,1)S(1)}, u32[]{:S(2)}, u32[]{:S(2)}) collective-permute-start(bf16[3,1,2,1024]{3,2,1,0:T(2,128)(2,1)S(1)} %pad_maximum_fusion.8), channel_id=1, source_target_pairs={{4,0},{8,4},{12,8},{16,12},{20,16},{24,20},{28,24},{5,1},{9,5},{13... | collective-permute-start | bytes 36872 | tf_op jit(solution)/shard_map/ppermute | solution.py:32
  44.5 4.3 %collective-permute-done.6 = bf16[3,1,2,1024]{3,2,1,0:T(2,128)(2,1)S(1)} collective-permute-done((bf16[3,1,2,1024]{3,2,1,0:T(2,128)(2,1)S(1)}, bf16[3,1,2,1024]{3,2,1,0:T(2,128)(2,1)S(1)}, u32[]{:S(2)}, u32[]{:S(2)}) %collective-permute-start.6) | collective-permute-done | bytes 12320 | tf_op jit(solution)/shard_map/ppermute | solution.py:31
  48.8 3.7 %collective-permute-done.7 = bf16[3,1,2,1024]{3,2,1,0:T(2,128)(2,1)S(1)} collective-permute-done((bf16[3,1,2,1024]{3,2,1,0:T(2,128)(2,1)S(1)}, bf16[3,1,2,1024]{3,2,1,0:T(2,128)(2,1)S(1)}, u32[]{:S(2)}, u32[]{:S(2)}) %collective-permute-start.7) | collective-permute-done | bytes 12320 | tf_op jit(solution)/shard_map/ppermute | solution.py:32
  52.6 2.0 %copy.63 = bf16[2,9216]{0,1:T(8,128)(2,1)} copy(bf16[2,9216]{1,0:T(2,128)(2,1)S(1)} %bitcast.152) | data formatting | bytes 73728 | tf_op jit(solution)/shard_map/while | solution.py:101
  55.5 1.5 %pad_maximum_fusion = bf16[3,3,1024,128]{3,2,1,0:T(8,128)(2,1)S(1)} fusion(bf16[3,1,1024,128]{3,2,1,0:T(8,128)(2,1)} %collective-permute-done.3, bf16[1,1,1024,128]{3,2,1,0:T(8,128)(2,1)S(1)} %collective-permute-done.1, bf16[1,1,1024,128]{3,2,1,0:T(8,128)(2,1)S(1)} %slice_bitcast_fusion.11, bf16[1,1,1024,128]{3,2,1,0:T(8,128)(2,1)S(1)} %collective-permute-done, ...), kind=kLoop, calls=%fused_computation.15 | loop fusion | flops 4718592 | bytes 4718592 | tf_op jit(solution)/shard_map/concatenate | solution.py:33
  57.1 10.6 %while.12 = (s32[]{:T(128)}, f32[4,128,128]{2,1,0:T(8,128)S(1)}, f32[4,128]{1,0:T(4,128)S(1)}, s32[]{:T(128)}, s32[4,256]{1,0:T(4,128)S(1)}, /*index=5*/bf16[921...) while((s32[]{:T(128)}, f32[4,128,128]{2,1,0:T(8,128)S(1)}, ...), condition=%wide.region_3.4_spmd, body=%wide.region_2.3_spmd.sunk | while | flops 101652616 | bytes 1486023 | solution.py:101
  57.1 3.0 %gather_fusion.1 = bf16[512,2]{1,0:T(8,128)(2,1)S(1)} fusion(bf16[2,9216]{0,1:T(8,128)(2,1)} %get-tuple-element.193, s32[1024]{0:T(1024)S(1)} %pad_clamp_fusion.2), kind=kCustom, calls=%fused_computation.1.clone.1 | custom fusion | bytes 6144 | tf_op jit(solution)/shard_map/while/body/gather | solution.py:85
  60.3 1.3 %gather_fusion = bf16[512,128]{1,0:T(8,128)(2,1)S(1)} fusion(bf16[9216,128]{1,0:T(8,128)(2,1)S(1)} %get-tuple-element.191, s32[1024]{0:T(1024)S(1)} %pad_clamp_fusion.2), kind=kCustom, calls=%fused_computation.clone.1 | custom fusion | bytes 264192 | tf_op jit(solution)/shard_map/while/body/gather | solution.py:84
  62.4 3.0 %gather_fusion.1 = bf16[512,2]{1,0:T(8,128)(2,1)S(1)} fusion(bf16[2,9216]{0,1:T(8,128)(2,1)} %get-tuple-element.193, s32[1024]{0:T(1024)S(1)} %pad_clamp_fusion.2), kind=kCustom, calls=%fused_computation.1.clone.1 | custom fusion | bytes 6144 | tf_op jit(solution)/shard_map/while/body/gather | solution.py:85
  65.6 1.3 %gather_fusion = bf16[512,128]{1,0:T(8,128)(2,1)S(1)} fusion(bf16[9216,128]{1,0:T(8,128)(2,1)S(1)} %get-tuple-element.191, s32[1024]{0:T(1024)S(1)} %pad_clamp_fusion.2), kind=kCustom, calls=%fused_computation.clone.1 | custom fusion | bytes 264192 | tf_op jit(solution)/shard_map/while/body/gather | solution.py:84
  73.6 3.0 %collective-permute-start.9 = (bf16[1,1,128,128]{3,2,1,0:T(8,128)(2,1)S(1)}, bf16[1,1,128,128]{3,2,1,0:T(8,128)(2,1)S(1)}, u32[]{:S(2)}, u32[]{:S(2)}) collective-permute-start(bf16[1,1,128,128]{3,2,1,0:T(8,128)(2,1)S(1)} %get-tuple-element.91), channel_id=1, source_target_pairs={{32,0},{64,32},{96,64},{128,96},{160,128},{192,160},{224,192},{33,... | collective-permute-start | bytes 98312 | tf_op jit(solution)/shard_map/ppermute | solution.py:32
  76.7 2.8 %collective-permute-start.8 = (bf16[1,1,128,128]{3,2,0,1:T(8,128)(2,1)S(1)}, bf16[1,1,128,128]{3,2,0,1:T(8,128)(2,1)S(1)}, u32[]{:S(2)}, u32[]{:S(2)}) collective-permute-start(bf16[1,1,128,128]{3,2,0,1:T(8,128)(2,1)S(1)} %get-tuple-element.90), channel_id=1, source_target_pairs={{0,32},{32,64},{64,96},{96,128},{128,160},{160,192},{192,224},{1,3... | collective-permute-start | bytes 98312 | tf_op jit(solution)/shard_map/ppermute | solution.py:31
  79.7 4.9 %collective-permute-done.8 = bf16[1,1,128,128]{3,2,0,1:T(8,128)(2,1)S(1)} collective-permute-done((bf16[1,1,128,128]{3,2,0,1:T(8,128)(2,1)S(1)}, bf16[1,1,128,128]{3,2,0,1:T(8,128)(2,1)S(1)}, u32[]{:S(2)}, u32[]{:S(2)}) %collective-permute-start.8) | collective-permute-done | bytes 32800 | tf_op jit(solution)/shard_map/ppermute | solution.py:31
  84.6 5.0 %collective-permute-start.10 = (bf16[6,1,128,128]{3,2,0,1:T(8,128)(2,1)S(1)}, bf16[6,1,128,128]{3,2,0,1:T(8,128)(2,1)S(1)}, u32[]{:S(2)}, u32[]{:S(2)}) collective-permute-start(bf16[6,1,128,128]{3,2,0,1:T(8,128)(2,1)S(1)} %pad_maximum_fusion.5), channel_id=1, source_target_pairs={{0,4},{4,8},{8,12},{12,16},{16,20},{20,24},{24,28},{1,5},{5,9},{9,... | collective-permute-start | bytes 589832 | tf_op jit(solution)/shard_map/ppermute | solution.py:31
  89.6 2.1 %collective-permute-start.11 = (bf16[6,1,128,128]{3,2,0,1:T(8,128)(2,1)S(1)}, bf16[6,1,128,128]{3,2,0,1:T(8,128)(2,1)S(1)}, u32[]{:S(2)}, u32[]{:S(2)}) collective-permute-start(bf16[6,1,128,128]{3,2,0,1:T(8,128)(2,1)S(1)} %pad_maximum_fusion.5), channel_id=1, source_target_pairs={{4,0},{8,4},{12,8},{16,12},{20,16},{24,20},{28,24},{5,1},{9,5},{13... | collective-permute-start | bytes 589832 | tf_op jit(solution)/shard_map/ppermute | solution.py:32
  92.8 5.3 %collective-permute-done.11 = bf16[6,1,128,128]{3,2,0,1:T(8,128)(2,1)S(1)} collective-permute-done((bf16[6,1,128,128]{3,2,0,1:T(8,128)(2,1)S(1)}, bf16[6,1,128,128]{3,2,0,1:T(8,128)(2,1)S(1)}, u32[]{:S(2)}, u32[]{:S(2)}) %collective-permute-start.11) | collective-permute-done | bytes 196640 | tf_op jit(solution)/shard_map/ppermute | solution.py:32
  (100 shorter events, 21.5 us)
Async XLA Ops:
  0.0 27.5 %copy-start = (bf16[2,64,16,128]{3,2,1,0:T(8,128)(2,1)S(1)}, bf16[2,64,16,128]{3,2,1,0:T(8,128)(2,1)}, u32[]{:S(2)}) copy-start(bf16[2,64,16,128]{3,2,1,0:T(8,128)(2,1)} %param.10) | copy-start | bytes 1572868
  10.7 17.2 %collective-permute-start = (bf16[1,1,1024,128]{3,2,1,0:T(8,128)(2,1)S(1)}, bf16[1,1,1024,128]{3,2,1,0:T(8,128)(2,1)S(1)}, u32[]{:S(2)}, u32[]{:S(2)}) collective-permute-start(bf16[1,1,1024,128]{3,2,1,0:T(8,128)(2,1)S(1)} %slice_bitcast_fusion.11), channel_id=1, source_target_pairs={{0,32},{32,64},{64,96},{96,128},{128,160},{160,192},{192,224},{1,3... | collective-permute-start | bytes 786440 | tf_op jit(solution)/shard_map/ppermute | solution.py:31
  14.2 13.7 %collective-permute-start.1 = (bf16[1,1,1024,128]{3,2,1,0:T(8,128)(2,1)S(1)}, bf16[1,1,1024,128]{3,2,1,0:T(8,128)(2,1)S(1)}, u32[]{:S(2)}, u32[]{:S(2)}) collective-permute-start(bf16[1,1,1024,128]{3,2,1,0:T(8,128)(2,1)S(1)} %slice_bitcast_fusion.11), channel_id=1, source_target_pairs={{32,0},{64,32},{96,64},{128,96},{160,128},{192,160},{224,192},{33,... | collective-permute-start | bytes 786440 | tf_op jit(solution)/shard_map/ppermute | solution.py:32
  18.7 24.6 %copy-start.3 = (s32[4,1]{0,1:T(1,128)S(1)}, s32[4,1]{0,1:T(1,128)}, u32[]{:S(2)}) copy-start(s32[4,1]{0,1:T(1,128)} %param.16) | copy-start | bytes 52
  18.7 25.8 %copy-start.4 = (f32[4,1,256]{2,1,0:T(1,128)S(1)}, f32[4,1,256]{2,1,0:T(1,128)}, u32[]{:S(2)}) copy-start(f32[4,1,256]{2,1,0:T(1,128)} %param.17) | copy-start | bytes 12292
  18.7 16.5 %collective-permute-start.4 = (bf16[1,1,2,1024]{2,3,1,0:T(8,128)(2,1)S(1)}, bf16[1,1,2,1024]{2,3,1,0:T(8,128)(2,1)}, u32[]{:S(2)}, u32[]{:S(2)}) collective-permute-start(bf16[1,1,2,1024]{2,3,1,0:T(8,128)(2,1)S(1)} %slice_bitcast_fusion.10), channel_id=1, source_target_pairs={{0,32},{32,64},{64,96},{96,128},{128,160},{160,192},{192,224},{1,3... | collective-permute-start | bytes 12296 | tf_op jit(solution)/shard_map/ppermute | solution.py:31
  20.6 15.7 %collective-permute-start.5 = (bf16[1,1,2,1024]{2,3,1,0:T(8,128)(2,1)S(1)}, bf16[1,1,2,1024]{2,3,1,0:T(8,128)(2,1)}, u32[]{:S(2)}, u32[]{:S(2)}) collective-permute-start(bf16[1,1,2,1024]{2,3,1,0:T(8,128)(2,1)S(1)} %slice_bitcast_fusion.10), channel_id=1, source_target_pairs={{32,0},{64,32},{96,64},{128,96},{160,128},{192,160},{224,192},{33,... | collective-permute-start | bytes 12296 | tf_op jit(solution)/shard_map/ppermute | solution.py:32
  28.0 26.6 %collective-permute-start.2 = (bf16[3,1,1024,128]{3,2,1,0:T(8,128)(2,1)S(1)}, bf16[3,1,1024,128]{3,2,1,0:T(8,128)(2,1)S(1)}, u32[]{:S(2)}, u32[]{:S(2)}) collective-permute-start(bf16[3,1,1024,128]{3,2,1,0:T(8,128)(2,1)S(1)} %pad_maximum_fusion.1), channel_id=1, source_target_pairs={{0,4},{4,8},{8,12},{12,16},{16,20},{20,24},{24,28},{1,5},{5,9},{9,... | collective-permute-start | bytes 2359304 | tf_op jit(solution)/shard_map/ppermute | solution.py:31
  31.8 23.7 %collective-permute-start.3 = (bf16[3,1,1024,128]{3,2,1,0:T(8,128)(2,1)S(1)}, bf16[3,1,1024,128]{3,2,1,0:T(8,128)(2,1)}, u32[]{:S(2)}, u32[]{:S(2)}) collective-permute-start(bf16[3,1,1024,128]{3,2,1,0:T(8,128)(2,1)S(1)} %pad_maximum_fusion.1), channel_id=1, source_target_pairs={{4,0},{8,4},{12,8},{16,12},{20,16},{24,20},{28,24},{5,1},{9,5},{13... | collective-permute-start | bytes 2359304 | tf_op jit(solution)/shard_map/ppermute | solution.py:32
  37.4 11.4 %collective-permute-start.6 = (bf16[3,1,2,1024]{3,2,1,0:T(2,128)(2,1)S(1)}, bf16[3,1,2,1024]{3,2,1,0:T(2,128)(2,1)S(1)}, u32[]{:S(2)}, u32[]{:S(2)}) collective-permute-start(bf16[3,1,2,1024]{3,2,1,0:T(2,128)(2,1)S(1)} %pad_maximum_fusion.8), channel_id=1, source_target_pairs={{0,4},{4,8},{8,12},{12,16},{16,20},{20,24},{24,28},{1,5},{5,9},{9,... | collective-permute-start | bytes 36872 | tf_op jit(solution)/shard_map/ppermute | solution.py:31
  41.2 11.4 %collective-permute-start.7 = (bf16[3,1,2,1024]{3,2,1,0:T(2,128)(2,1)S(1)}, bf16[3,1,2,1024]{3,2,1,0:T(2,128)(2,1)S(1)}, u32[]{:S(2)}, u32[]{:S(2)}) collective-permute-start(bf16[3,1,2,1024]{3,2,1,0:T(2,128)(2,1)S(1)} %pad_maximum_fusion.8), channel_id=1, source_target_pairs={{4,0},{8,4},{12,8},{16,12},{20,16},{24,20},{28,24},{5,1},{9,5},{13... | collective-permute-start | bytes 36872 | tf_op jit(solution)/shard_map/ppermute | solution.py:32
  54.6 0.9 copy-start.1
  73.6 6.0 %collective-permute-start.9 = (bf16[1,1,128,128]{3,2,1,0:T(8,128)(2,1)S(1)}, bf16[1,1,128,128]{3,2,1,0:T(8,128)(2,1)S(1)}, u32[]{:S(2)}, u32[]{:S(2)}) collective-permute-start(bf16[1,1,128,128]{3,2,1,0:T(8,128)(2,1)S(1)} %get-tuple-element.91), channel_id=1, source_target_pairs={{32,0},{64,32},{96,64},{128,96},{160,128},{192,160},{224,192},{33,... | collective-permute-start | bytes 98312 | tf_op jit(solution)/shard_map/ppermute | solution.py:32
  76.7 7.9 %collective-permute-start.8 = (bf16[1,1,128,128]{3,2,0,1:T(8,128)(2,1)S(1)}, bf16[1,1,128,128]{3,2,0,1:T(8,128)(2,1)S(1)}, u32[]{:S(2)}, u32[]{:S(2)}) collective-permute-start(bf16[1,1,128,128]{3,2,0,1:T(8,128)(2,1)S(1)} %get-tuple-element.90), channel_id=1, source_target_pairs={{0,32},{32,64},{64,96},{96,128},{128,160},{160,192},{192,224},{1,3... | collective-permute-start | bytes 98312 | tf_op jit(solution)/shard_map/ppermute | solution.py:31
  84.6 8.2 %collective-permute-start.10 = (bf16[6,1,128,128]{3,2,0,1:T(8,128)(2,1)S(1)}, bf16[6,1,128,128]{3,2,0,1:T(8,128)(2,1)S(1)}, u32[]{:S(2)}, u32[]{:S(2)}) collective-permute-start(bf16[6,1,128,128]{3,2,0,1:T(8,128)(2,1)S(1)} %pad_maximum_fusion.5), channel_id=1, source_target_pairs={{0,4},{4,8},{8,12},{12,16},{16,20},{20,24},{24,28},{1,5},{5,9},{9,... | collective-permute-start | bytes 589832 | tf_op jit(solution)/shard_map/ppermute | solution.py:31
  89.6 8.5 %collective-permute-start.11 = (bf16[6,1,128,128]{3,2,0,1:T(8,128)(2,1)S(1)}, bf16[6,1,128,128]{3,2,0,1:T(8,128)(2,1)S(1)}, u32[]{:S(2)}, u32[]{:S(2)}) collective-permute-start(bf16[6,1,128,128]{3,2,0,1:T(8,128)(2,1)S(1)} %pad_maximum_fusion.5), channel_id=1, source_target_pairs={{4,0},{8,4},{12,8},{16,12},{20,16},{24,20},{28,24},{5,1},{9,5},{13... | collective-permute-start | bytes 589832 | tf_op jit(solution)/shard_map/ppermute | solution.py:32
  98.6 1.1 %copy-start.2 = (bf16[2,64,16,128]{3,2,1,0:T(8,128)(2,1)S(1)}, bf16[2,64,16,128]{3,2,1,0:T(8,128)(2,1)}, u32[]{:S(2)}) copy-start(bf16[2,64,16,128]{3,2,1,0:T(8,128)(2,1)} %fusion.17) | copy-start | bytes 1572868
where the time goes:
time: 103 us; the launch traced here: 102 us
  starting transfers between devices  40.6 us (39%)
  waiting for transfers between devices  19.3 us (19%)
  local copies, waits for them, and re-layouts  17.2 us (17%)
  blocking collectives  8.27 us (8%)
  other arithmetic  7.76 us (8%)
  matrix products  7.73 us (8%)
  between operations  1.12 us (1%)
    ppermute x6, starting transfers between devices, padded(): before = lax.ppermute(last, axis, up)  20.9 us
    ppermute x6, starting transfers between devices, padded(): after = lax.ppermute(initial, axis, down)  19.7 us
    ppermute x6, waiting for transfers between devices, padded(): before = lax.ppermute(last, axis, up)  10.2 us
    ppermute x6, waiting for transfers between devices, padded(): after = lax.ppermute(initial, axis, down)  9.08 us
    all_gather x1, blocking collectives, rows_first(): out = lax.all_gather(both, axis, axis=0, tiled=True)  8.27 us
    gather x4, local copies, waits for them, and re-layouts, add_block(): picked = flat_values[:, slot_rows]  6.26 us
    gather x4, local copies, waits for them, and re-layouts, add_block(): pert_rows = flat_pert[slot_rows].astype(jnp.float32)  2.95 us
  transfers between devices with their start and end apart: 12, of which 5 were waited for; matrix products, arithmetic and copies ran while one was open for 7% of the time, Pallas kernels for 0%

commit v1 on v0

v1 whole, which is shorter than its diff:
```python
import functools

import jax
import jax.numpy as jnp
from jax import lax
from jax.experimental import pallas as pl
from jax.experimental.pallas import tpu as pltpu
from jax.sharding import PartitionSpec as P

SPACING = 16
NS_STEPS = 4
MESH = pl.DeviceIdType.MESH
F32 = jnp.float32
BF16 = jnp.bfloat16
NT = (((1,), (1,)), ((), ()))

STEPS = ((0, 1), (0, -1), (1, 0), (-1, 0), (1, 1), (1, -1), (-1, 1), (-1, -1))


def halves(value):
    high = value.astype(BF16)
    return high, (value - high.astype(F32)).astype(BF16)


def product(left, right):
    left_high, left_low = left
    right_high, right_low = right
    return jnp.dot(
        jnp.concatenate([left_high, left_high, left_low], axis=1),
        jnp.concatenate([right_high, right_low, right_high], axis=0),
        preferred_element_type=F32,
    )


def solve(gram, proj_rows):
    members = gram.shape[0]
    spread = float(members - 1)
    rows = lax.broadcasted_iota(jnp.int32, gram.shape, 0)
    columns = lax.broadcasted_iota(jnp.int32, gram.shape, 1)
    diagonal = rows == columns
    square = jnp.sum(jnp.sum(gram * gram, axis=0, keepdims=True), axis=1, keepdims=True)
    norm = spread + jnp.sqrt(square)
    base = (jnp.where(diagonal, spread, 0.0) + gram) * (1.0 / norm)
    middle = jnp.where(diagonal, 1.5, 0.0) - 0.5 * base
    split_middle = halves(middle)
    root = product(halves(base), split_middle)
    inverse = middle
    target = jnp.broadcast_to(proj_rows[0:1, :], gram.shape).T
    for step in range(1, NS_STEPS):
        split_inverse = halves(inverse)
        split_root = halves(root)
        middle = jnp.where(diagonal, 1.5, 0.0) - 0.5 * product(split_inverse, split_root)
        split_middle = halves(middle)
        if step < NS_STEPS - 1:
            root = product(split_root, split_middle)
        else:
            target = product(split_inverse, halves(target))
        inverse = product(split_middle, split_inverse)
    inner = product(split_middle, halves(target))
    mean_weights = product(halves(inverse), halves(inner)) * (1.0 / norm)
    transform = (jnp.sqrt(spread) * lax.rsqrt(norm)) * inverse + mean_weights
    return transform.astype(BF16)


def kernel(
    tiles_x,
    tiles_y,
    members_ref,
    obs_ref,
    innovation_ref,
    precision_ref,
    owner_ref,
    slot_ref,
    count_ref,
    local_ref,
    out_ref,
    members_v,
    pert_v,
    mean_v,
    obs_v,
    near_v,
    scalar_v,
    owner_v,
    slot_v,
    count_v,
    local_v,
    dense_v,
    gram_v,
    from_core_v,
    sum_v,
    from_chip_v,
    weights_v,
    load_sem,
    obs_send,
    obs_recv,
    scalar_send,
    scalar_recv,
    gram_send,
    gram_recv,
    weight_send,
    weight_recv,
    pass_send,
    pass_recv,
):
    tx = lax.axis_index("tx")
    ty = lax.axis_index("ty")
    lev = lax.axis_index("lev")
    core = lev % 2
    own_obs, member_count = obs_ref.shape
    blocks = own_obs // 128
    columns = owner_ref.shape[0]
    slots = owner_ref.shape[2]

    def exists(dx, dy):
        x, y = tx + dx, ty + dy
        return (x >= 0) & (x < tiles_x) & (y >= 0) & (y < tiles_y)

    loads = [
        pltpu.make_async_copy(source, target, load_sem.at[k])
        for k, (source, target) in enumerate(
            (
                (obs_ref, obs_v),
                (owner_ref, owner_v),
                (slot_ref, slot_v),
                (count_ref, count_v),
                (local_ref, local_v),
                (precision_ref, scalar_v.at[4, 0]),
                (innovation_ref, scalar_v.at[4, 1]),
                (members_ref, members_v),
            )
        )
    ]
    for load in loads:
        load.start()

    barrier = pltpu.get_barrier_semaphore()
    other_core = (tx, ty, lev + 1 - 2 * core)
    other_chip = (tx, ty, (lev + 2) % 4)
    for dx, dy in STEPS:

        @pl.when(exists(dx, dy))
        def _():
            pl.semaphore_signal(
                barrier, inc=1, device_id=(tx + dx, ty + dy, lev), device_id_type=MESH
            )

    pl.semaphore_signal(barrier, inc=1, device_id=other_core, device_id_type=MESH)
    pl.semaphore_signal(barrier, inc=1, device_id=other_chip, device_id_type=MESH)

    loads[0].wait()
    near_v[4] = obs_v[...].astype(F32).T.astype(BF16)
    for load in loads[1:7]:
        load.wait()

    reach_x = 1 + (tx > 0).astype(jnp.int32) + (tx < tiles_x - 1).astype(jnp.int32)
    reach_y = 1 + (ty > 0).astype(jnp.int32) + (ty < tiles_y - 1).astype(jnp.int32)
    pl.semaphore_wait(barrier, reach_x * reach_y - 1 + 2)

    def obs_copies(dx, dy):
        theirs = (1 - dx) * 3 + (1 - dy)
        return tuple(
            pltpu.make_async_remote_copy(
                src_ref=buffer.at[4],
                dst_ref=buffer.at[theirs],
                send_sem=send.at[theirs],
                recv_sem=recv.at[theirs],
                device_id=(tx + dx, ty + dy, lev),
                device_id_type=MESH,
            )
            for buffer, send, recv in (
                (scalar_v, scalar_send, scalar_recv),
                (near_v, obs_send, obs_recv),
            )
        )

    for dx, dy in STEPS:

        @pl.when(exists(dx, dy))
        def _():
            for copy in obs_copies(dx, dy):
                copy.start()

    keys, lanes, parts = [], [], []
    position = lax.broadcasted_iota(jnp.int32, (1, slots), 1)
    quarter = own_obs
    for c in range(columns):
        owner = owner_v[c]
        slot = slot_v[c]
        near_x = owner // tiles_y - tx + 1
        near_y = owner % tiles_y - ty + 1
        block = (near_x * 3 + near_y) * blocks + (slot % quarter) // 128
        live = (position < count_v[c : c + 1, :]) & (slot // quarter == lev)
        keys.append(jnp.where(live, block * 8 + c, -1))
        lanes.append(slot % 128)
        parts.append(local_v[c])
    key = jnp.concatenate(keys, axis=1)
    lane = jnp.concatenate(lanes, axis=1)
    local = jnp.concatenate(parts, axis=1)
    high = local.astype(BF16).astype(F32)
    middle = (local - high).astype(BF16).astype(F32)
    low = local - high - middle
    dense_rows = 9 * blocks * 8
    row = lax.broadcasted_iota(jnp.int32, (dense_rows, columns * slots), 0)
    chosen = row == key
    spot = (lax.broadcasted_iota(jnp.int32, (128, columns * slots), 0) == lane).astype(F32)
    spot = spot.astype(BF16)
    dense = 0.0
    for part in (low, middle, high):
        dense += lax.dot_general(
            jnp.where(chosen, part, 0.0).astype(BF16), spot, NT, preferred_element_type=F32
        )
    dense_v[...] = dense.reshape(9 * blocks, 8, 128)

    gram_v[...] = jnp.zeros_like(gram_v)

    def add_block(near):
        turned = near_v[near]
        wide = turned.astype(F32)
        scalars = scalar_v[near].astype(F32)
        weight = jnp.concatenate(
            [dense_v[near * blocks + h] * scalars[0, h : h + 1, :] for h in range(blocks)], axis=1
        )
        departure = jnp.concatenate([scalars[1, h : h + 1, :] for h in range(blocks)], axis=1)
        for c in range(columns):
            upper, lower = halves(wide * weight[c : c + 1, :])
            gram_v[c, 0:member_count, :] += lax.dot_general(
                upper, turned, NT, preferred_element_type=F32
            ) + lax.dot_general(lower, turned, NT, preferred_element_type=F32)
        upper, lower = halves(weight * departure)
        shares = lax.dot_general(
            upper, turned, NT, preferred_element_type=F32
        ) + lax.dot_general(lower, turned, NT, preferred_element_type=F32)
        for c in range(columns):
            gram_v[c, member_count : member_count + 8, :] += jnp.broadcast_to(
                shares[c : c + 1, :], (8, member_count)
            )

    add_block(4)

    loads[7].wait()
    averaging = jnp.full((member_count, member_count), 1.0 / member_count, BF16)
    level_count, width_x, width_y, _ = members_v.shape
    for level in range(level_count):
        for first in range(0, width_x, 32):
            states = members_v[level, first : first + 32].reshape(32 * width_y, member_count)
            mean = jnp.dot(states, averaging, preferred_element_type=F32)
            mean_v[level, first : first + 32] = mean.reshape(32, width_y, member_count)
            pert_v[level, first : first + 32] = (
                (states.astype(F32) - mean).astype(BF16).reshape(32, width_y, member_count)
            )

    for dx, dy in STEPS:

        @pl.when(exists(dx, dy))
        def _():
            near = (1 + dx) * 3 + (1 + dy)
            for copy in obs_copies(-dx, -dy):
                copy.wait_recv()
            add_block(near)

    mine, others = 2 * core, 2 - 2 * core
    to_core = pltpu.make_async_remote_copy(
        src_ref=gram_v.at[pl.ds(others, 2)],
        dst_ref=from_core_v,
        send_sem=gram_send.at[0],
        recv_sem=gram_recv.at[0],
        device_id=other_core,
        device_id_type=MESH,
    )
    to_core.start()
    to_core.wait_recv()
    sum_v[...] = gram_v[pl.ds(mine, 2)] + from_core_v[...]
    to_chip = pltpu.make_async_remote_copy(
        src_ref=sum_v,
        dst_ref=from_chip_v,
        send_sem=gram_send.at[1],
        recv_sem=gram_recv.at[1],
        device_id=other_chip,
        device_id_type=MESH,
    )
    to_chip.start()
    to_chip.wait_recv()
    for k in range(2):
        gram = sum_v[k, 0:member_count] + from_chip_v[k, 0:member_count]
        proj = sum_v[k, member_count:] + from_chip_v[k, member_count:]
        weights_v[1, 1 + mine + k] = solve(gram, proj)

    outward = 2 * core - 1
    rim_from = 1 + 3 * core
    rim_to = 5 - 5 * core

    def pass_copy(index, ref):
        return pltpu.make_async_remote_copy(
            src_ref=ref,
            dst_ref=ref,
            send_sem=pass_send.at[index],
            recv_sem=pass_recv.at[index],
            device_id=other_core,
            device_id_type=MESH,
        )

    def pair(y, first):
        return weights_v.at[y, pl.ds(first, 2)]

    pair_mine, pair_other = 1 + mine, 1 + others
    rim_mine, rim_other = rim_to, 5 - rim_to

    def pair_copy(e):
        return pltpu.make_async_remote_copy(
            src_ref=pair(1, pair_mine),
            dst_ref=pair(1 - e, pair_mine),
            send_sem=weight_send.at[1 - e],
            recv_sem=weight_recv.at[1 - e],
            device_id=(tx, ty + e, lev),
            device_id_type=MESH,
        )

    def rim_copy(e, sign):
        return pltpu.make_async_remote_copy(
            src_ref=weights_v.at[1, rim_from],
            dst_ref=weights_v.at[1 - e, rim_mine],
            send_sem=weight_send.at[4 - e],
            recv_sem=weight_recv.at[4 - e],
            device_id=(tx + sign * outward, ty + e, lev),
            device_id_type=MESH,
        )

    for e in (1, -1):

        @pl.when(exists(0, e))
        def _():
            pair_copy(e).start()

    for e in (1, -1, 0):

        @pl.when(exists(outward, e))
        def _():
            rim_copy(e, 1).start()

    pass_copy(1, pair(1, pair_mine)).start()
    for e in (0, 1, -1):
        if e:

            @pl.when(exists(0, -e))
            def _():
                pair_copy(e).wait_recv()
                pass_copy(1 - e, pair(1 - e, pair_mine)).start()

        @pl.when(exists(-outward, -e))
        def _():
            rim_copy(e, 1).wait_recv()
            pass_copy(4 - e, weights_v.at[1 - e, rim_mine]).start()

    pass_copy(1, pair(1, pair_other)).wait_recv()
    for e in (0, 1, -1):
        if e:

            @pl.when(exists(0, -e))
            def _():
                pass_copy(1 - e, pair(1 - e, pair_other)).wait_recv()

        @pl.when(exists(outward, -e))
        def _():
            pass_copy(4 - e, weights_v.at[1 - e, rim_other]).wait_recv()

    half_span = SPACING // 2
    places_y = [jnp.where(ty == 0, 1, 0), 1, jnp.where(ty == tiles_y - 1, 1, 2)]
    places_x = [jnp.where(tx == 0, 1, 0), 1, 2, 3, 4, jnp.where(tx == tiles_x - 1, 4, 5)]
    within = lax.broadcasted_iota(jnp.int32, (half_span, member_count), 0).astype(F32)
    upper_y = [(within + half_span + 0.5) / SPACING, (within + 0.5) / SPACING]
    for patch in range(width_x // half_span):
        left = (patch + 1) // 2
        corners = jnp.concatenate(
            [weights_v[y, x] for x in (places_x[left], places_x[left + 1]) for y in places_y],
            axis=1,
        )
        first = patch * half_span
        pert = pert_v[:, first : first + half_span].reshape(-1, member_count)
        mixed = jnp.dot(pert, corners, preferred_element_type=F32)
        mixed = mixed.reshape(level_count, half_span, width_y, 6 * member_count)
        for level in range(level_count):
            for x in range(half_span):
                fx = (x + 0.5 + (half_span if patch % 2 == 0 else 0)) / SPACING
                sides = []
                for p in range(2):
                    fy = upper_y[p]
                    rows = mixed[level, x, p * half_span : (p + 1) * half_span]
                    total = mean_v[level, first + x, p * half_span : (p + 1) * half_span]
                    for u in range(2):
                        for v in range(2):
                            at = (u * 3 + p + v) * member_count
                            factor = (fx if u else 1.0 - fx) * (fy if v else 1.0 - fy)
                            total = total + rows[:, at : at + member_count] * factor
                    sides.append(total)
                out_ref[level, first + x] = jnp.concatenate(sides, axis=0).astype(BF16)

    for dx, dy in STEPS:

        @pl.when(exists(dx, dy))
        def _():
            for copy in obs_copies(dx, dy):
                copy.wait_send()

    to_core.wait_send()
    to_chip.wait_send()
    pass_copy(1, pair(1, pair_mine)).wait_send()
    for e in (0, 1, -1):
        if e:

            @pl.when(exists(0, e))
            def _():
                pair_copy(e).wait_send()

            @pl.when(exists(0, -e))
            def _():
                pass_copy(1 - e, pair(1 - e, pair_mine)).wait_send()

        @pl.when(exists(outward, e))
        def _():
            rim_copy(e, 1).wait_send()

        @pl.when(exists(-outward, -e))
        def _():
            pass_copy(4 - e, weights_v.at[1 - e, rim_mine]).wait_send()


def per_device(
    tiles_x,
    tiles_y,
    members,
    obs_pert,
    innovation,
    obs_precision,
    obs_owner,
    obs_slot,
    obs_count,
    local_weight,
):
    own_obs, member_count = obs_pert.shape
    blocks = own_obs // 128
    anywhere = pl.BlockSpec(memory_space=pl.ANY)
    dma = pltpu.SemaphoreType.DMA
    return pl.pallas_call(
        functools.partial(kernel, tiles_x, tiles_y),
        out_shape=jax.ShapeDtypeStruct(members.shape, BF16),
        in_specs=[anywhere] * 8,
        out_specs=pl.BlockSpec(memory_space=pltpu.VMEM),
        scratch_shapes=[
            pltpu.VMEM(members.shape, BF16),
            pltpu.VMEM(members.shape, BF16),
            pltpu.VMEM(members.shape, F32),
            pltpu.VMEM(obs_pert.shape, BF16),
            pltpu.VMEM((9, member_count, own_obs), BF16),
            pltpu.VMEM((9, 2, blocks, 128), BF16),
            pltpu.VMEM(obs_owner.shape, jnp.int32),
            pltpu.VMEM(obs_slot.shape, jnp.int32),
            pltpu.VMEM(obs_count.shape, jnp.int32),
            pltpu.VMEM(local_weight.shape, F32),
            pltpu.VMEM((9 * blocks, 8, 128), F32),
            pltpu.VMEM((4, member_count + 8, member_count), F32),
            pltpu.VMEM((2, member_count + 8, member_count), F32),
            pltpu.VMEM((2, member_count + 8, member_count), F32),
            pltpu.VMEM((2, member_count + 8, member_count), F32),
            pltpu.VMEM((3, 6, member_count, member_count), BF16),
            dma((8,)),
            dma((9,)),
            dma((9,)),
            dma((9,)),
            dma((9,)),
            dma((2,)),
            dma((2,)),
            dma((6,)),
            dma((6,)),
            dma((6,)),
            dma((6,)),
        ],
        compiler_params=pltpu.CompilerParams(
            collective_id=0, has_side_effects=True, vmem_limit_bytes=48 * 1024 * 1024
        ),
    )(
        members,
        obs_pert,
        innovation.reshape(blocks, 128),
        obs_precision.reshape(blocks, 128),
        obs_owner,
        obs_slot,
        obs_count,
        local_weight,
    )


def solution(mesh):
    placed = (
        P("lev", "tx", "ty", None),
        P(("tx", "ty", "lev"), None),
        P(("tx", "ty", "lev")),
        P(("tx", "ty", "lev")),
        P("tx", "ty", None),
        P("tx", "ty", None),
        P("tx", "ty"),
        P("tx", "ty", None),
    )
    return jax.shard_map(
        functools.partial(per_device, mesh.shape["tx"], mesh.shape["ty"]),
        mesh=mesh,
        in_specs=placed,
        out_specs=P("lev", "tx", "ty", None),
        check_vma=False,
    )
```

time: 103 us -> 38.7 us (0.38)
  starting transfers between devices: 40.6 us -> 0 us
  Pallas kernels: 0 us -> 33.6 us
  waiting for transfers between devices: 19.3 us -> 0 us
  local copies, waits for them, and re-layouts: 17.2 us -> 4.83 us
  blocking collectives: 8.27 us -> 0 us
  other arithmetic: 7.76 us -> 0 us
  matrix products: 7.73 us -> 0 us
  between operations: 1.12 us -> 0.03 us
    ppermute x12 -> x0, starting transfers between devices: 40.6 us -> none  [the longest x6 20.9 us: padded(): before = lax.ppermute(last, axis, up)]
    pallas_call x0 -> x1, Pallas kernels: none -> 33.6 us  [per_device(): pl.pallas_call(functools.partial(kernel, tiles_x, tiles_y), out_shape=jax...]
    ppermute x12 -> x0, waiting for transfers between devices: 19.3 us -> none  [the longest x6 10.2 us: padded(): before = lax.ppermute(last, axis, up)]
    gather x8 -> x0, local copies, waits for them, and re-layouts: 9.21 us -> none  [the longest x4 6.26 us: add_block(): picked = flat_values[:, slot_rows]]
    all_gather x1 -> x0, blocking collectives: 8.27 us -> none  [rows_first(): out = lax.all_gather(both, axis, axis=0, tiled=True)]
    dot_general x21 -> x0, matrix products: 7.73 us -> none  [the longest x4 1.66 us: finish_solve(): jnp.einsum('bij,bjk->bik', inv_iter, sqrt_iter, precision=lax.Precision.H...]
    unnamed x11 -> x16, local copies, waits for them, and re-layouts: 0.93 us -> 4.83 us
    concatenate x9 -> x0, other arithmetic: 2.79 us -> none  [the longest x6 1.79 us: padded(): array = jnp.concatenate([before, array, after], axis=dim)]
  transfers between devices with their start and end apart: 12 -> 0, of which waited for: 5 -> 0; matrix products, arithmetic and copies ran while one was open for 7% -> 0% of each run, Pallas kernels for 0% -> 0%
where the time goes in v1:
time: 38.7 us; the launch traced here: 38.4 us
  Pallas kernels  33.6 us (87%)
  local copies, waits for them, and re-layouts  4.83 us (12%)
    pallas_call x1, Pallas kernels, per_device(): pl.pallas_call(functools.partial(kernel, tiles_x, tiles_y), out_shape=jax...  33.6 us
    unnamed x16, local copies, waits for them, and re-layouts  4.83 us

profile of v1, /device:TPU:34, one launch (start us, length us, event | category | flops | bytes accessed | tf_op | source)
XLA Modules:
  0.0 38.4 jit_solution(13869885378895303550)
XLA Ops:
  0.0 0.0 copy-start.2
  0.0 0.0 copy-start.5
  0.0 0.0 copy-start.6
  0.0 0.8 %copy.9.count_ref = s32[4,1]{1,0:T(4,128)S(1)} copy(s32[4,1]{0,1:T(1,128)} %param.14) | data formatting | bytes 32 | tf_op args[6]
  0.8 0.0 copy-done.2
  0.8 0.0 copy-done.5
  0.8 0.0 copy-done.6
  0.8 0.0 copy-start
  0.8 1.0 %copy-done = bf16[2,64,16,128]{3,2,1,0:T(8,128)(2,1)S(1)} copy-done((bf16[2,64,16,128]{3,2,1,0:T(8,128)(2,1)S(1)}, bf16[2,64,16,128]{3,2,1,0:T(8,128)(2,1)}, u32[]{:S(2)}) %copy-start) | copy-done | bytes 524312
  1.8 0.0 copy-start.1
  1.8 0.8 %copy-done.1 = bf16[256,128]{1,0:T(8,128)(2,1)S(1)} copy-done((bf16[256,128]{1,0:T(8,128)(2,1)S(1)}, bf16[256,128]{1,0:T(8,128)(2,1)}, u32[]{:S(2)}) %copy-start.1) | copy-done | bytes 65560
  2.7 0.0 copy-start.3
  2.7 0.7 %copy-done.3 = s32[4,1,256]{2,1,0:T(1,128)S(1)} copy-done((s32[4,1,256]{2,1,0:T(1,128)S(1)}, s32[4,1,256]{2,1,0:T(1,128)}, u32[]{:S(2)}) %copy-start.3) | copy-done | bytes 4120
  3.4 0.0 copy-start.4
  3.4 0.7 %copy-done.4 = f32[4,1,256]{2,1,0:T(1,128)S(1)} copy-done((f32[4,1,256]{2,1,0:T(1,128)S(1)}, f32[4,1,256]{2,1,0:T(1,128)}, u32[]{:S(2)}) %copy-start.4) | copy-done | bytes 4120
  4.1 33.6 %shard_map.82 = bf16[2,64,16,128]{3,2,1,0:T(8,128)(2,1)S(1)} custom-call(bf16[2,64,16,128]{3,2,1,0:T(8,128)(2,1)S(1)} %copy-done, bf16[256,128]{1,0:T(8,128)(2,1)S(1)} %copy-done.1, bf16[2,128]{1,0:T(2,128)(2,1)S(1)} %bitcast.2, bf16[2,128]{1,0:T(2,128)(2,1)S(1)} %bitcast.3, s32[4,1,256]{2,1,0:T(1,128)S(1)} %copy-done.2, s32[4,1,256]{2,1,0:T(1,128)S(1)} %copy-done.3, ...), custom_call_target="tpu_custom_call" | custom-call | tf_op jit(solution)/shard_map/pallas_call | solution.py:443
  37.6 0.8 %copy.11 = bf16[2,64,16,128]{3,2,1,0:T(8,128)(2,1)} copy(bf16[2,64,16,128]{3,2,1,0:T(8,128)(2,1)S(1)} %shard_map.82) | data formatting | bytes 1048576
Async XLA Ops:
  0.0 0.8 %copy-start.2 = (s32[4,1,256]{2,1,0:T(1,128)S(1)}, s32[4,1,256]{2,1,0:T(1,128)}, u32[]{:S(2)}) copy-start(s32[4,1,256]{2,1,0:T(1,128)} %owner_ref.1) | copy-start | bytes 12292
  0.0 0.8 %copy-start.5 = (bf16[256]{0:T(256)(128)(2,1)S(1)}, bf16[256]{0:T(256)(128)(2,1)}, u32[]{:S(2)}) copy-start(bf16[256]{0:T(256)(128)(2,1)} %param.10) | copy-start | bytes 1540
  0.0 0.8 %copy-start.6 = (bf16[256]{0:T(256)(128)(2,1)S(1)}, bf16[256]{0:T(256)(128)(2,1)}, u32[]{:S(2)}) copy-start(bf16[256]{0:T(256)(128)(2,1)} %param.11) | copy-start | bytes 1540
  0.8 1.0 %copy-start = (bf16[2,64,16,128]{3,2,1,0:T(8,128)(2,1)S(1)}, bf16[2,64,16,128]{3,2,1,0:T(8,128)(2,1)}, u32[]{:S(2)}) copy-start(bf16[2,64,16,128]{3,2,1,0:T(8,128)(2,1)} %members_ref.1) | copy-start | bytes 1572868
  1.8 0.8 %copy-start.1 = (bf16[256,128]{1,0:T(8,128)(2,1)S(1)}, bf16[256,128]{1,0:T(8,128)(2,1)}, u32[]{:S(2)}) copy-start(bf16[256,128]{1,0:T(8,128)(2,1)} %obs_ref.1) | copy-start | bytes 196612
  2.7 0.7 %copy-start.3 = (s32[4,1,256]{2,1,0:T(1,128)S(1)}, s32[4,1,256]{2,1,0:T(1,128)}, u32[]{:S(2)}) copy-start(s32[4,1,256]{2,1,0:T(1,128)} %slot_ref.1) | copy-start | bytes 12292
  3.4 0.7 %copy-start.4 = (f32[4,1,256]{2,1,0:T(1,128)S(1)}, f32[4,1,256]{2,1,0:T(1,128)}, u32[]{:S(2)}) copy-start(f32[4,1,256]{2,1,0:T(1,128)} %local_ref.1) | copy-start | bytes 12292

commit v2 on v1

--- a/solution.py
+++ b/solution.py
@@ -15,6 +15,7 @@
 NT = (((1,), (1,)), ((), ()))
 
 STEPS = ((0, 1), (0, -1), (1, 0), (-1, 0), (1, 1), (1, -1), (-1, 1), (-1, -1))
+GROUPS = (STEPS[:4], STEPS[4:])
 
 
 def halves(value):
@@ -40,10 +41,14 @@
     diagonal = rows == columns
     square = jnp.sum(jnp.sum(gram * gram, axis=0, keepdims=True), axis=1, keepdims=True)
     norm = spread + jnp.sqrt(square)
-    base = (jnp.where(diagonal, spread, 0.0) + gram) * (1.0 / norm)
+    raised = jnp.where(diagonal, spread, 0.0) + gram
+    split_raised = halves(raised)
+    squared = product(split_raised, split_raised)
+    scale = 1.0 / norm
+    base = raised * scale
     middle = jnp.where(diagonal, 1.5, 0.0) - 0.5 * base
     split_middle = halves(middle)
-    root = product(halves(base), split_middle)
+    root = 1.5 * base - squared * (0.5 * scale * scale)
     inverse = middle
     target = jnp.broadcast_to(proj_rows[0:1, :], gram.shape).T
     for step in range(1, NS_STEPS):
@@ -57,7 +62,7 @@
             target = product(split_inverse, halves(target))
         inverse = product(split_middle, split_inverse)
     inner = product(split_middle, halves(target))
-    mean_weights = product(halves(inverse), halves(inner)) * (1.0 / norm)
+    mean_weights = product(halves(inverse), halves(inner)) * scale
     transform = (jnp.sqrt(spread) * lax.rsqrt(norm)) * inverse + mean_weights
     return transform.astype(BF16)
 
@@ -88,6 +93,7 @@
     gram_v,
     from_core_v,
     sum_v,
+    half_v,
     from_chip_v,
     weights_v,
     load_sem,
@@ -136,6 +142,7 @@
     barrier = pltpu.get_barrier_semaphore()
     other_core = (tx, ty, lev + 1 - 2 * core)
     other_chip = (tx, ty, (lev + 2) % 4)
+    far_core = (tx, ty, 3 - lev)
     for dx, dy in STEPS:
 
         @pl.when(exists(dx, dy))
@@ -144,8 +151,29 @@
                 barrier, inc=1, device_id=(tx + dx, ty + dy, lev), device_id_type=MESH
             )
 
+    outward = 2 * core - 1
+    for e in (-1, 0, 1):
+
+        @pl.when(exists(outward, e))
+        def _():
+            pl.semaphore_signal(
+                barrier,
+                inc=1,
+                device_id=(tx + outward, ty + e, lev + 1 - 2 * core),
+                device_id_type=MESH,
+            )
+
     pl.semaphore_signal(barrier, inc=1, device_id=other_core, device_id_type=MESH)
     pl.semaphore_signal(barrier, inc=1, device_id=other_chip, device_id_type=MESH)
+    pl.semaphore_signal(barrier, inc=1, device_id=far_core, device_id_type=MESH)
+
+    for dx, dy in STEPS:
+
+        @pl.when(jnp.logical_not(exists(dx, dy)))
+        def _():
+            near = (1 + dx) * 3 + (1 + dy)
+            near_v[near] = jnp.zeros(near_v.shape[1:], BF16)
+            scalar_v[near] = jnp.zeros(scalar_v.shape[1:], BF16)
 
     loads[0].wait()
     near_v[4] = obs_v[...].astype(F32).T.astype(BF16)
@@ -154,7 +182,8 @@
 
     reach_x = 1 + (tx > 0).astype(jnp.int32) + (tx < tiles_x - 1).astype(jnp.int32)
     reach_y = 1 + (ty > 0).astype(jnp.int32) + (ty < tiles_y - 1).astype(jnp.int32)
-    pl.semaphore_wait(barrier, reach_x * reach_y - 1 + 2)
+    crossing = exists(outward, 0).astype(jnp.int32) * reach_y
+    pl.semaphore_wait(barrier, reach_x * reach_y - 1 + crossing + 3)
 
     def obs_copies(dx, dy):
         theirs = (1 - dx) * 3 + (1 - dy)
@@ -189,7 +218,7 @@
         near_x = owner // tiles_y - tx + 1
         near_y = owner % tiles_y - ty + 1
         block = (near_x * 3 + near_y) * blocks + (slot % quarter) // 128
-        live = (position < count_v[c : c + 1, :]) & (slot // quarter == lev)
+        live = (position < count_v[:, c : c + 1]) & (slot // quarter == lev)
         keys.append(jnp.where(live, block * 8 + c, -1))
         lanes.append(slot % 128)
         parts.append(local_v[c])
@@ -213,29 +242,40 @@
 
     gram_v[...] = jnp.zeros_like(gram_v)
 
-    def add_block(near):
-        turned = near_v[near]
-        wide = turned.astype(F32)
-        scalars = scalar_v[near].astype(F32)
-        weight = jnp.concatenate(
-            [dense_v[near * blocks + h] * scalars[0, h : h + 1, :] for h in range(blocks)], axis=1
-        )
-        departure = jnp.concatenate([scalars[1, h : h + 1, :] for h in range(blocks)], axis=1)
+    def add_blocks(nears):
+        left, right = [], []
+        for near in nears:
+            turned = near_v[near]
+            wide = turned.astype(F32)
+            scalars = scalar_v[near].astype(F32)
+            weight = jnp.concatenate(
+                [dense_v[near * blocks + h] * scalars[0, h : h + 1, :] for h in range(blocks)],
+                axis=1,
+            )
+            departure = jnp.concatenate([scalars[1, h : h + 1, :] for h in range(blocks)], axis=1)
+            pairs = [halves(wide * weight[c : c + 1, :]) for c in range(columns)]
+            pairs.append(halves(weight * departure))
+            left.append(jnp.concatenate([half for pair in pairs for half in pair], axis=0))
+            right.append(turned)
+        sums = lax.dot_general(
+            jnp.concatenate(left, axis=1),
+            jnp.concatenate(right, axis=1),
+            NT,
+            preferred_element_type=F32,
+        )
+        at = 0
         for c in range(columns):
-            upper, lower = halves(wide * weight[c : c + 1, :])
-            gram_v[c, 0:member_count, :] += lax.dot_general(
-                upper, turned, NT, preferred_element_type=F32
-            ) + lax.dot_general(lower, turned, NT, preferred_element_type=F32)
-        upper, lower = halves(weight * departure)
-        shares = lax.dot_general(
-            upper, turned, NT, preferred_element_type=F32
-        ) + lax.dot_general(lower, turned, NT, preferred_element_type=F32)
+            gram_v[c, 0:member_count, :] += (
+                sums[at : at + member_count] + sums[at + member_count : at + 2 * member_count]
+            )
+            at += 2 * member_count
+        shares = sums[at : at + 8] + sums[at + 8 : at + 16]
         for c in range(columns):
             gram_v[c, member_count : member_count + 8, :] += jnp.broadcast_to(
                 shares[c : c + 1, :], (8, member_count)
             )
 
-    add_block(4)
+    add_blocks([4])
 
     loads[7].wait()
     averaging = jnp.full((member_count, member_count), 1.0 / member_count, BF16)
@@ -249,43 +289,49 @@
                 (states.astype(F32) - mean).astype(BF16).reshape(32, width_y, member_count)
             )
 
-    for dx, dy in STEPS:
-
-        @pl.when(exists(dx, dy))
-        def _():
-            near = (1 + dx) * 3 + (1 + dy)
-            for copy in obs_copies(-dx, -dy):
-                copy.wait_recv()
-            add_block(near)
+    for group in GROUPS:
+        for dx, dy in group:
+
+            @pl.when(exists(dx, dy))
+            def _():
+                for copy in obs_copies(-dx, -dy):
+                    copy.wait_recv()
+
+        add_blocks([(1 + dx) * 3 + (1 + dy) for dx, dy in group])
 
     mine, others = 2 * core, 2 - 2 * core
-    to_core = pltpu.make_async_remote_copy(
-        src_ref=gram_v.at[pl.ds(others, 2)],
-        dst_ref=from_core_v,
-        send_sem=gram_send.at[0],
-        recv_sem=gram_recv.at[0],
-        device_id=other_core,
-        device_id_type=MESH,
-    )
+    for c in range(columns):
+        half_v[c, 0:member_count] = gram_v[c, 0:member_count].astype(BF16)
+        half_v[c, member_count:] = jnp.concatenate(halves(gram_v[c, member_count:]), axis=0)
+
+    def gram_copy(index, source, target, where):
+        return pltpu.make_async_remote_copy(
+            src_ref=source,
+            dst_ref=target,
+            send_sem=gram_send.at[index],
+            recv_sem=gram_recv.at[index],
+            device_id=where,
+            device_id_type=MESH,
+        )
+
+    to_core = gram_copy(0, gram_v.at[pl.ds(others, 2)], from_core_v, other_core)
+    to_chip = gram_copy(1, half_v.at[pl.ds(mine, 2)], from_chip_v.at[0], other_chip)
+    to_far = gram_copy(2, half_v.at[pl.ds(others, 2)], from_chip_v.at[1], far_core)
+    to_far.start()
+    to_chip.start()
     to_core.start()
     to_core.wait_recv()
     sum_v[...] = gram_v[pl.ds(mine, 2)] + from_core_v[...]
-    to_chip = pltpu.make_async_remote_copy(
-        src_ref=sum_v,
-        dst_ref=from_chip_v,
-        send_sem=gram_send.at[1],
-        recv_sem=gram_recv.at[1],
-        device_id=other_chip,
-        device_id_type=MESH,
-    )
-    to_chip.start()
     to_chip.wait_recv()
+    to_far.wait_recv()
     for k in range(2):
-        gram = sum_v[k, 0:member_count] + from_chip_v[k, 0:member_count]
-        proj = sum_v[k, member_count:] + from_chip_v[k, member_count:]
+        theirs = from_chip_v[0, k].astype(F32) + from_chip_v[1, k].astype(F32)
+        gram = sum_v[k, 0:member_count] + theirs[0:member_count]
+        upper = theirs[member_count : member_count + 8]
+        lower = theirs[member_count + 8 : member_count + 16]
+        proj = sum_v[k, member_count:] + (upper + lower)
         weights_v[1, 1 + mine + k] = solve(gram, proj)
 
-    outward = 2 * core - 1
     rim_from = 1 + 3 * core
     rim_to = 5 - 5 * core
 
@@ -315,13 +361,15 @@
             device_id_type=MESH,
         )
 
-    def rim_copy(e, sign):
+    def rim_copy(e, across):
+        where = (tx + outward, ty + e, lev + across * (1 - 2 * core))
+        index = 3 + 3 * across + 1 - e
         return pltpu.make_async_remote_copy(
             src_ref=weights_v.at[1, rim_from],
             dst_ref=weights_v.at[1 - e, rim_mine],
-            send_sem=weight_send.at[4 - e],
-            recv_sem=weight_recv.at[4 - e],
-            device_id=(tx + sign * outward, ty + e, lev),
+            send_sem=weight_send.at[index],
+            recv_sem=weight_recv.at[index],
+            device_id=where,
             device_id_type=MESH,
         )
 
@@ -335,33 +383,40 @@
 
         @pl.when(exists(outward, e))
         def _():
+            rim_copy(e, 0).start()
             rim_copy(e, 1).start()
 
     pass_copy(1, pair(1, pair_mine)).start()
+    for e in (1, -1):
+
+        @pl.when(exists(0, -e))
+        def _():
+            pair_copy(e).wait_recv()
+            pass_copy(1 - e, pair(1 - e, pair_mine)).start()
+
+    pass_copy(1, pair(1, pair_other)).wait_recv()
+    for e in (1, -1):
+
+        @pl.when(exists(0, -e))
+        def _():
+            pass_copy(1 - e, pair(1 - e, pair_other)).wait_recv()
+
     for e in (0, 1, -1):
-        if e:
-
-            @pl.when(exists(0, -e))
-            def _():
-                pair_copy(e).wait_recv()
-                pass_copy(1 - e, pair(1 - e, pair_mine)).start()
 
         @pl.when(exists(-outward, -e))
         def _():
-            rim_copy(e, 1).wait_recv()
-            pass_copy(4 - e, weights_v.at[1 - e, rim_mine]).start()
-
-    pass_copy(1, pair(1, pair_other)).wait_recv()
-    for e in (0, 1, -1):
-        if e:
-
-            @pl.when(exists(0, -e))
-            def _():
-                pass_copy(1 - e, pair(1 - e, pair_other)).wait_recv()
+            rim_copy(e, 0).wait_recv()
 
         @pl.when(exists(outward, -e))
         def _():
-            pass_copy(4 - e, weights_v.at[1 - e, rim_other]).wait_recv()
+            pltpu.make_async_remote_copy(
+                src_ref=weights_v.at[1, rim_from],
+                dst_ref=weights_v.at[1 - e, rim_other],
+                send_sem=weight_send.at[7 - e],
+                recv_sem=weight_recv.at[7 - e],
+                device_id=other_core,
+                device_id_type=MESH,
+            ).wait_recv()
 
     half_span = SPACING // 2
     places_y = [jnp.where(ty == 0, 1, 0), 1, jnp.where(ty == tiles_y - 1, 1, 2)]
@@ -403,6 +458,7 @@
 
     to_core.wait_send()
     to_chip.wait_send()
+    to_far.wait_send()
     pass_copy(1, pair(1, pair_mine)).wait_send()
     for e in (0, 1, -1):
         if e:
@@ -417,11 +473,8 @@
 
         @pl.when(exists(outward, e))
         def _():
+            rim_copy(e, 0).wait_send()
             rim_copy(e, 1).wait_send()
-
-        @pl.when(exists(-outward, -e))
-        def _():
-            pass_copy(4 - e, weights_v.at[1 - e, rim_mine]).wait_send()
 
 
 def per_device(
@@ -438,7 +491,7 @@
 ):
     own_obs, member_count = obs_pert.shape
     blocks = own_obs // 128
-    anywhere = pl.BlockSpec(memory_space=pl.ANY)
+    anywhere = pl.BlockSpec(memory_space=pltpu.HBM)
     dma = pltpu.SemaphoreType.DMA
     return pl.pallas_call(
         functools.partial(kernel, tiles_x, tiles_y),
@@ -454,38 +507,41 @@
             pltpu.VMEM((9, 2, blocks, 128), BF16),
             pltpu.VMEM(obs_owner.shape, jnp.int32),
             pltpu.VMEM(obs_slot.shape, jnp.int32),
-            pltpu.VMEM(obs_count.shape, jnp.int32),
+            pltpu.VMEM((1, obs_count.size), jnp.int32),
             pltpu.VMEM(local_weight.shape, F32),
             pltpu.VMEM((9 * blocks, 8, 128), F32),
             pltpu.VMEM((4, member_count + 8, member_count), F32),
             pltpu.VMEM((2, member_count + 8, member_count), F32),
             pltpu.VMEM((2, member_count + 8, member_count), F32),
-            pltpu.VMEM((2, member_count + 8, member_count), F32),
+            pltpu.VMEM((4, member_count + 16, member_count), BF16),
+            pltpu.VMEM((2, 2, member_count + 16, member_count), BF16),
             pltpu.VMEM((3, 6, member_count, member_count), BF16),
             dma((8,)),
             dma((9,)),
             dma((9,)),
             dma((9,)),
             dma((9,)),
-            dma((2,)),
-            dma((2,)),
-            dma((6,)),
-            dma((6,)),
-            dma((6,)),
-            dma((6,)),
+            dma((3,)),
+            dma((3,)),
+            dma((9,)),
+            dma((9,)),
+            dma((3,)),
+            dma((3,)),
         ],
         compiler_params=pltpu.CompilerParams(
             collective_id=0, has_side_effects=True, vmem_limit_bytes=48 * 1024 * 1024
         ),
     )(
+        *(pltpu.with_memory_space_constraint(x, pltpu.HBM) for x in (
         members,
         obs_pert,
         innovation.reshape(blocks, 128),
         obs_precision.reshape(blocks, 128),
         obs_owner,
         obs_slot,
-        obs_count,
+        obs_count.reshape(1, -1),
         local_weight,
+        ))
     )
 
 

time: 38.7 us -> 31.8 us (0.82)
  local copies, waits for them, and re-layouts: 4.83 us -> 0.8 us
  Pallas kernels: 33.6 us -> 30.9 us
    unnamed x16 -> x1, local copies, waits for them, and re-layouts: 4.83 us -> 0.8 us
    pallas_call x1, Pallas kernels: 33.6 us -> 30.9 us  [per_device(): pl.pallas_call(functools.partial(kernel, tiles_x, tiles_y), out_shape=jax...]
where the time goes in v2:
time: 31.8 us; the launch traced here: 31.7 us
  Pallas kernels  30.9 us (97%)
  local copies, waits for them, and re-layouts  0.8 us (3%)
    pallas_call x1, Pallas kernels, per_device(): pl.pallas_call(functools.partial(kernel, tiles_x, tiles_y), out_shape=jax...  30.9 us
    unnamed x1, local copies, waits for them, and re-layouts  0.8 us

profile of v2, /device:TPU:34, one launch (start us, length us, event | category | flops | bytes accessed | tf_op | source)
XLA Modules:
  0.0 31.7 jit_solution(7512919496970735333)
XLA Ops:
  0.0 30.9 %shard_map.82 = bf16[2,64,16,128]{3,2,1,0:T(8,128)(2,1)S(1)} custom-call(bf16[2,64,16,128]{3,2,1,0:T(8,128)(2,1)} %members_ref.1, bf16[256,128]{1,0:T(8,128)(2,1)} %obs_ref.1, bf16[2,128]{1,0:T(2,128)(2,1)} %bitcast.3, bf16[2,128]{1,0:T(2,128)(2,1)} %bitcast.4, s32[4,1,256]{2,1,0:T(1,128)} %owner_ref.1, s32[4,1,256]{2,1,0:T(1,128)} %slot_ref.1, ...), custom_call_target="tpu_custom_call" | custom-call | tf_op jit(solution)/shard_map/pallas_call | solution.py:496
  30.9 0.8 %copy.10 = bf16[2,64,16,128]{3,2,1,0:T(8,128)(2,1)} copy(bf16[2,64,16,128]{3,2,1,0:T(8,128)(2,1)S(1)} %shard_map.82) | data formatting | bytes 1048576

commit v3 on v2

--- a/solution.py
+++ b/solution.py
@@ -14,8 +14,8 @@
 BF16 = jnp.bfloat16
 NT = (((1,), (1,)), ((), ()))
 
-STEPS = ((0, 1), (0, -1), (1, 0), (-1, 0), (1, 1), (1, -1), (-1, 1), (-1, -1))
-GROUPS = (STEPS[:4], STEPS[4:])
+STEPS = ((1, 1), (1, -1), (-1, 1), (-1, -1), (0, 1), (0, -1), (1, 0), (-1, 0))
+GROUPS = (STEPS,)
 
 
 def halves(value):
@@ -31,6 +31,10 @@
         jnp.concatenate([right_high, right_low, right_high], axis=0),
         preferred_element_type=F32,
     )
+
+
+def beside(left, right):
+    return tuple(jnp.concatenate(pair, axis=1) for pair in zip(left, right))
 
 
 def solve(gram, proj_rows):
@@ -46,22 +50,21 @@
     squared = product(split_raised, split_raised)
     scale = 1.0 / norm
     base = raised * scale
-    middle = jnp.where(diagonal, 1.5, 0.0) - 0.5 * base
-    split_middle = halves(middle)
+    three_halves = jnp.where(diagonal, 1.5, 0.0)
+    inverse = three_halves - 0.5 * base
     root = 1.5 * base - squared * (0.5 * scale * scale)
-    inverse = middle
     target = jnp.broadcast_to(proj_rows[0:1, :], gram.shape).T
     for step in range(1, NS_STEPS):
-        split_inverse = halves(inverse)
-        split_root = halves(root)
-        middle = jnp.where(diagonal, 1.5, 0.0) - 0.5 * product(split_inverse, split_root)
-        split_middle = halves(middle)
+        split_inverse, split_root = halves(inverse), halves(root)
         if step < NS_STEPS - 1:
-            root = product(split_root, split_middle)
+            middle = three_halves - 0.5 * product(split_inverse, split_root)
+            both = product(halves(middle), beside(split_root, split_inverse))
+            root, inverse = both[:, :members], both[:, members:]
         else:
-            target = product(split_inverse, halves(target))
-        inverse = product(split_middle, split_inverse)
-    inner = product(split_middle, halves(target))
+            both = product(split_inverse, beside(split_root, halves(target)))
+            middle = three_halves - 0.5 * both[:, :members]
+            both = product(halves(middle), beside(split_inverse, halves(both[:, members:])))
+            inverse, inner = both[:, :members], both[:, members:]
     mean_weights = product(halves(inverse), halves(inner)) * scale
     transform = (jnp.sqrt(spread) * lax.rsqrt(norm)) * inverse + mean_weights
     return transform.astype(BF16)
@@ -253,7 +256,7 @@
                 axis=1,
             )
             departure = jnp.concatenate([scalars[1, h : h + 1, :] for h in range(blocks)], axis=1)
-            pairs = [halves(wide * weight[c : c + 1, :]) for c in range(columns)]
+            pairs = [((wide * weight[c : c + 1, :]).astype(BF16),) for c in range(columns)]
             pairs.append(halves(weight * departure))
             left.append(jnp.concatenate([half for pair in pairs for half in pair], axis=0))
             right.append(turned)
@@ -265,10 +268,8 @@
         )
         at = 0
         for c in range(columns):
-            gram_v[c, 0:member_count, :] += (
-                sums[at : at + member_count] + sums[at + member_count : at + 2 * member_count]
-            )
-            at += 2 * member_count
+            gram_v[c, 0:member_count, :] += sums[at : at + member_count]
+            at += member_count
         shares = sums[at : at + 8] + sums[at + 8 : at + 16]
         for c in range(columns):
             gram_v[c, member_count : member_count + 8, :] += jnp.broadcast_to(
@@ -278,6 +279,7 @@
     add_blocks([4])
 
     loads[7].wait()
+    half_span = SPACING // 2
     averaging = jnp.full((member_count, member_count), 1.0 / member_count, BF16)
     level_count, width_x, width_y, _ = members_v.shape
     for level in range(level_count):
@@ -285,9 +287,10 @@
             states = members_v[level, first : first + 32].reshape(32 * width_y, member_count)
             mean = jnp.dot(states, averaging, preferred_element_type=F32)
             mean_v[level, first : first + 32] = mean.reshape(32, width_y, member_count)
-            pert_v[level, first : first + 32] = (
-                (states.astype(F32) - mean).astype(BF16).reshape(32, width_y, member_count)
-            )
+            pert = (states.astype(F32) - mean).reshape(32, width_y, member_count)
+            for p in range(2):
+                half = pert[:, p * half_span : (p + 1) * half_span].reshape(-1, member_count)
+                pert_v[p, level, first * half_span : (first + 32) * half_span] = half.astype(BF16)
 
     for group in GROUPS:
         for dx, dy in group:
@@ -387,6 +390,70 @@
             rim_copy(e, 1).start()
 
     pass_copy(1, pair(1, pair_mine)).start()
+    places_y = [jnp.where(ty == 0, 1, 0), 1, jnp.where(ty == tiles_y - 1, 1, 2)]
+    places_x = [jnp.where(tx == 0, 1, 0), 1, 2, 3, 4, jnp.where(tx == tiles_x - 1, 4, 5)]
+    patches = width_x // half_span
+    within = lax.broadcasted_iota(jnp.int32, (half_span, member_count), 0).astype(F32)
+    upper_y = [(within + half_span + 0.5) / SPACING, (within + 0.5) / SPACING]
+    centre_y = [upper_y[0], 1.0 - upper_y[1]]
+    outer_y = [1.0 - upper_y[0], upper_y[1]]
+
+    def part_x(patch, x, u):
+        fx = (x + 0.5 + (half_span if patch % 2 == 0 else 0)) / SPACING
+        return fx if u else 1.0 - fx
+
+    def mix(patch, p, places):
+        first = patch * half_span * half_span
+        states = pert_v[p, :, first : first + half_span * half_span].reshape(-1, member_count)
+        corners = jnp.concatenate([weights_v[y, x] for y, x in places], axis=1)
+        mixed = jnp.dot(states, corners, preferred_element_type=F32)
+        return mixed.reshape(level_count, half_span, half_span, len(places) * member_count)
+
+    def add_centre(patch):
+        left = (patch + 1) // 2
+        sides = [u for u in range(2) if 1 <= left + u <= 4]
+        for p in range(2):
+            mixed = mix(patch, p, [(1, left + u) for u in sides])
+            for level in range(level_count):
+                for x in range(half_span):
+                    at = (level, patch * half_span + x, slice(p * half_span, (p + 1) * half_span))
+                    total = mean_v[at]
+                    for i, u in enumerate(sides):
+                        share = mixed[level, x, :, i * member_count : (i + 1) * member_count]
+                        total = total + share * (part_x(patch, x, u) * centre_y[p])
+                    mean_v[at] = total
+
+    def finish(patch):
+        left = (patch + 1) // 2
+        rims = [u for u in range(2) if not 1 <= left + u <= 4]
+        mixed = [
+            mix(
+                patch,
+                p,
+                [(places_y[2 * p], places_x[left + u]) for u in range(2)]
+                + [(1, places_x[left + u]) for u in rims],
+            )
+            for p in range(2)
+        ]
+        for level in range(level_count):
+            for x in range(half_span):
+                sides = []
+                for p in range(2):
+                    total = mean_v[
+                        level, patch * half_span + x, p * half_span : (p + 1) * half_span
+                    ]
+                    factors = [part_x(patch, x, u) * outer_y[p] for u in range(2)]
+                    factors += [part_x(patch, x, u) * centre_y[p] for u in rims]
+                    for i, factor in enumerate(factors):
+                        share = mixed[p][level, x, :, i * member_count : (i + 1) * member_count]
+                        total = total + share * factor
+                    sides.append(total)
+                out_ref[level, patch * half_span + x] = jnp.concatenate(sides, axis=0).astype(BF16)
+
+    pass_copy(1, pair(1, pair_other)).wait_recv()
+    for patch in range(patches):
+        add_centre(patch)
+
     for e in (1, -1):
 
         @pl.when(exists(0, -e))
@@ -394,12 +461,14 @@
             pair_copy(e).wait_recv()
             pass_copy(1 - e, pair(1 - e, pair_mine)).start()
 
-    pass_copy(1, pair(1, pair_other)).wait_recv()
     for e in (1, -1):
 
         @pl.when(exists(0, -e))
         def _():
             pass_copy(1 - e, pair(1 - e, pair_other)).wait_recv()
+
+    for patch in range(1, patches - 1):
+        finish(patch)
 
     for e in (0, 1, -1):
 
@@ -418,36 +487,8 @@
                 device_id_type=MESH,
             ).wait_recv()
 
-    half_span = SPACING // 2
-    places_y = [jnp.where(ty == 0, 1, 0), 1, jnp.where(ty == tiles_y - 1, 1, 2)]
-    places_x = [jnp.where(tx == 0, 1, 0), 1, 2, 3, 4, jnp.where(tx == tiles_x - 1, 4, 5)]
-    within = lax.broadcasted_iota(jnp.int32, (half_span, member_count), 0).astype(F32)
-    upper_y = [(within + half_span + 0.5) / SPACING, (within + 0.5) / SPACING]
-    for patch in range(width_x // half_span):
-        left = (patch + 1) // 2
-        corners = jnp.concatenate(
-            [weights_v[y, x] for x in (places_x[left], places_x[left + 1]) for y in places_y],
-            axis=1,
-        )
-        first = patch * half_span
-        pert = pert_v[:, first : first + half_span].reshape(-1, member_count)
-        mixed = jnp.dot(pert, corners, preferred_element_type=F32)
-        mixed = mixed.reshape(level_count, half_span, width_y, 6 * member_count)
-        for level in range(level_count):
-            for x in range(half_span):
-                fx = (x + 0.5 + (half_span if patch % 2 == 0 else 0)) / SPACING
-                sides = []
-                for p in range(2):
-                    fy = upper_y[p]
-                    rows = mixed[level, x, p * half_span : (p + 1) * half_span]
-                    total = mean_v[level, first + x, p * half_span : (p + 1) * half_span]
-                    for u in range(2):
-                        for v in range(2):
-                            at = (u * 3 + p + v) * member_count
-                            factor = (fx if u else 1.0 - fx) * (fy if v else 1.0 - fy)
-                            total = total + rows[:, at : at + member_count] * factor
-                    sides.append(total)
-                out_ref[level, first + x] = jnp.concatenate(sides, axis=0).astype(BF16)
+    finish(0)
+    finish(patches - 1)
 
     for dx, dy in STEPS:
 
@@ -500,7 +541,7 @@
         out_specs=pl.BlockSpec(memory_space=pltpu.VMEM),
         scratch_shapes=[
             pltpu.VMEM(members.shape, BF16),
-            pltpu.VMEM(members.shape, BF16),
+            pltpu.VMEM((2, members.shape[0], members.shape[1] * SPACING // 2, member_count), BF16),
             pltpu.VMEM(members.shape, F32),
             pltpu.VMEM(obs_pert.shape, BF16),
             pltpu.VMEM((9, member_count, own_obs), BF16),

time: 31.8 us -> 30 us (0.943)
  Pallas kernels: 30.9 us -> 28.8 us
    pallas_call x1, Pallas kernels: 30.9 us -> 28.8 us  [per_device(): pl.pallas_call(functools.partial(kernel, tiles_x, tiles_y), out_shape=jax...]
where the time goes in v3:
time: 30 us; the launch traced here: 29.6 us
  Pallas kernels  28.8 us (96%)
  local copies, waits for them, and re-layouts  0.8 us (3%)
    pallas_call x1, Pallas kernels, per_device(): pl.pallas_call(functools.partial(kernel, tiles_x, tiles_y), out_shape=jax...  28.8 us
    unnamed x1, local copies, waits for them, and re-layouts  0.8 us

profile of v3, /device:TPU:34, one launch (start us, length us, event | category | flops | bytes accessed | tf_op | source)
XLA Modules:
  0.0 29.6 jit_solution(9292367775995424487)
XLA Ops:
  0.0 28.8 %shard_map.82 = bf16[2,64,16,128]{3,2,1,0:T(8,128)(2,1)S(1)} custom-call(bf16[2,64,16,128]{3,2,1,0:T(8,128)(2,1)} %members_ref.1, bf16[256,128]{1,0:T(8,128)(2,1)} %obs_ref.1, bf16[2,128]{1,0:T(2,128)(2,1)} %bitcast.3, bf16[2,128]{1,0:T(2,128)(2,1)} %bitcast.4, s32[4,1,256]{2,1,0:T(1,128)} %owner_ref.1, s32[4,1,256]{2,1,0:T(1,128)} %slot_ref.1, ...), custom_call_target="tpu_custom_call" | custom-call | tf_op jit(solution)/shard_map/pallas_call | solution.py:537
  28.8 0.8 %copy.10 = bf16[2,64,16,128]{3,2,1,0:T(8,128)(2,1)} copy(bf16[2,64,16,128]{3,2,1,0:T(8,128)(2,1)S(1)} %shard_map.82) | data formatting | bytes 1048576

commit v4 on v3

--- a/solution.py
+++ b/solution.py
@@ -37,37 +37,61 @@
     return tuple(jnp.concatenate(pair, axis=1) for pair in zip(left, right))
 
 
-def solve(gram, proj_rows):
-    members = gram.shape[0]
+def products(lefts, rights):
+    return [product(left, right) for left, right in zip(lefts, rights)]
+
+
+def split(values):
+    return [halves(value) for value in values]
+
+
+def solve(grams, proj_rows):
+    shape = grams[0].shape
+    members = shape[0]
     spread = float(members - 1)
-    rows = lax.broadcasted_iota(jnp.int32, gram.shape, 0)
-    columns = lax.broadcasted_iota(jnp.int32, gram.shape, 1)
+    rows = lax.broadcasted_iota(jnp.int32, shape, 0)
+    columns = lax.broadcasted_iota(jnp.int32, shape, 1)
     diagonal = rows == columns
-    square = jnp.sum(jnp.sum(gram * gram, axis=0, keepdims=True), axis=1, keepdims=True)
-    norm = spread + jnp.sqrt(square)
-    raised = jnp.where(diagonal, spread, 0.0) + gram
-    split_raised = halves(raised)
-    squared = product(split_raised, split_raised)
-    scale = 1.0 / norm
-    base = raised * scale
     three_halves = jnp.where(diagonal, 1.5, 0.0)
-    inverse = three_halves - 0.5 * base
-    root = 1.5 * base - squared * (0.5 * scale * scale)
-    target = jnp.broadcast_to(proj_rows[0:1, :], gram.shape).T
+    raised = [jnp.where(diagonal, spread, 0.0) + gram for gram in grams]
+    split_raised = split(raised)
+    squares = [
+        jnp.sum(jnp.sum(gram * gram, axis=0, keepdims=True), axis=1, keepdims=True)
+        for gram in grams
+    ]
+    squared = products(split_raised, split_raised)
+    norms = [spread + jnp.sqrt(square) for square in squares]
+    scales = [1.0 / norm for norm in norms]
+    bases = [value * scale for value, scale in zip(raised, scales)]
+    inverses = [three_halves - 0.5 * base for base in bases]
+    roots = [
+        1.5 * base - square * (0.5 * scale * scale)
+        for base, square, scale in zip(bases, squared, scales)
+    ]
+    targets = [jnp.broadcast_to(proj[0:1, :], shape).T for proj in proj_rows]
     for step in range(1, NS_STEPS):
-        split_inverse, split_root = halves(inverse), halves(root)
+        split_inverses, split_roots = split(inverses), split(roots)
         if step < NS_STEPS - 1:
-            middle = three_halves - 0.5 * product(split_inverse, split_root)
-            both = product(halves(middle), beside(split_root, split_inverse))
-            root, inverse = both[:, :members], both[:, members:]
+            between = products(split_inverses, split_roots)
+            middles = [three_halves - 0.5 * value for value in between]
+            seconds = [beside(r, i) for r, i in zip(split_roots, split_inverses)]
+            both = products(split(middles), seconds)
+            roots = [value[:, :members] for value in both]
+            inverses = [value[:, members:] for value in both]
         else:
-            both = product(split_inverse, beside(split_root, halves(target)))
-            middle = three_halves - 0.5 * both[:, :members]
-            both = product(halves(middle), beside(split_inverse, halves(both[:, members:])))
-            inverse, inner = both[:, :members], both[:, members:]
-    mean_weights = product(halves(inverse), halves(inner)) * scale
-    transform = (jnp.sqrt(spread) * lax.rsqrt(norm)) * inverse + mean_weights
-    return transform.astype(BF16)
+            seconds = [beside(r, t) for r, t in zip(split_roots, split(targets))]
+            both = products(split_inverses, seconds)
+            middles = [three_halves - 0.5 * value[:, :members] for value in both]
+            mapped = split([value[:, members:] for value in both])
+            seconds = [beside(i, t) for i, t in zip(split_inverses, mapped)]
+            both = products(split(middles), seconds)
+            inverses = [value[:, :members] for value in both]
+            inners = [value[:, members:] for value in both]
+    means = products(split(inverses), split(inners))
+    return [
+        ((jnp.sqrt(spread) * lax.rsqrt(norm)) * inverse + mean * scale).astype(BF16)
+        for norm, inverse, mean, scale in zip(norms, inverses, means, scales)
+    ]
 
 
 def kernel(
@@ -327,13 +351,17 @@
     sum_v[...] = gram_v[pl.ds(mine, 2)] + from_core_v[...]
     to_chip.wait_recv()
     to_far.wait_recv()
+    grams, projs = [], []
     for k in range(2):
         theirs = from_chip_v[0, k].astype(F32) + from_chip_v[1, k].astype(F32)
         gram = sum_v[k, 0:member_count] + theirs[0:member_count]
         upper = theirs[member_count : member_count + 8]
         lower = theirs[member_count + 8 : member_count + 16]
         proj = sum_v[k, member_count:] + (upper + lower)
-        weights_v[1, 1 + mine + k] = solve(gram, proj)
+        grams.append(gram)
+        projs.append(proj)
+    for k, weights in enumerate(solve(grams, projs)):
+        weights_v[1, 1 + mine + k] = weights
 
     rim_from = 1 + 3 * core
     rim_to = 5 - 5 * core

time: 30 us -> 28.8 us (0.960)
  Pallas kernels: 28.8 us -> 27.6 us
    pallas_call x1, Pallas kernels: 28.8 us -> 27.6 us  [per_device(): pl.pallas_call(functools.partial(kernel, tiles_x, tiles_y), out_shape=jax...]
where the time goes in v4:
time: 28.8 us; the launch traced here: 28.4 us
  Pallas kernels  27.6 us (96%)
  local copies, waits for them, and re-layouts  0.8 us (3%)
    pallas_call x1, Pallas kernels, per_device(): pl.pallas_call(functools.partial(kernel, tiles_x, tiles_y), out_shape=jax...  27.6 us
    unnamed x1, local copies, waits for them, and re-layouts  0.8 us

profile of v4, /device:TPU:34, one launch (start us, length us, event | category | flops | bytes accessed | tf_op | source)
XLA Modules:
  0.0 28.4 jit_solution(11221034615178998557)
XLA Ops:
  0.0 27.6 %shard_map.82 = bf16[2,64,16,128]{3,2,1,0:T(8,128)(2,1)S(1)} custom-call(bf16[2,64,16,128]{3,2,1,0:T(8,128)(2,1)} %members_ref.1, bf16[256,128]{1,0:T(8,128)(2,1)} %obs_ref.1, bf16[2,128]{1,0:T(2,128)(2,1)} %bitcast.3, bf16[2,128]{1,0:T(2,128)(2,1)} %bitcast.4, s32[4,1,256]{2,1,0:T(1,128)} %owner_ref.1, s32[4,1,256]{2,1,0:T(1,128)} %slot_ref.1, ...), custom_call_target="tpu_custom_call" | custom-call | tf_op jit(solution)/shard_map/pallas_call | solution.py:565
  27.6 0.8 %copy.10 = bf16[2,64,16,128]{3,2,1,0:T(8,128)(2,1)} copy(bf16[2,64,16,128]{3,2,1,0:T(8,128)(2,1)S(1)} %shard_map.82) | data formatting | bytes 1048576
